TPU v7x, 32 devices: a whole 2x2x4 slice. The times are simulated.
32 devices in a mesh: dp: 8 (over y, x, core), tensor: 4 (over z).
Axes of the slice: x: 2, y: 2, z: 4, core: 2. Of those that a mesh axis runs over, the one named last changes fastest.
Arguments:
- hidden_in: bfloat16 [8192, 2048], P(('dp', 'tensor')), may hold values from -6 to 6
- norm_gains: bfloat16 [4, 2048], P(None, ('dp', 'tensor')), may hold values from 0.5 to 1.5
- q_weight: bfloat16 [2048, 2048], P('dp', 'tensor'), may hold values from -0.125 to 0.125
- k_weight: bfloat16 [2048, 2048], P('dp', 'tensor'), may hold values from -0.125 to 0.125
- v_weight: bfloat16 [2048, 2048], P('dp', 'tensor'), may hold values from -0.125 to 0.125
- o_weight: bfloat16 [2048, 2048], P('tensor', 'dp'), may hold values from -2 to 2
- gate_weight: bfloat16 [16, 2048, 1024], P(None, 'dp', 'tensor'), may hold values from -0.125 to 0.125
- up_weight: bfloat16 [16, 2048, 1024], P(None, 'dp', 'tensor'), may hold values from -0.125 to 0.125
- down_weight: bfloat16 [16, 1024, 2048], P(None, 'tensor', 'dp'), may hold values from -0.1875 to 0.1875
- lengths: int32 [8], P('dp'), may hold values from 1 to 1024, 7424 in all
- routes: int32 [8192, 8], P('dp'), may hold values from 0 to 15, all different within a row; in each aligned block of 1024 rows (0 to 1023, 1024 to 2047, ...) at most 768 rows name the same one
- route_weights: float32 [8192, 8], P('dp'), may hold values from 0.03 to 0.4
- out_grad: bfloat16 [8192, 2048], P(('dp', 'tensor')), may hold values from -6 to 6
Outputs:
- block_out: bfloat16 [8192, 2048], P(('dp', 'tensor'))
- input_grad: float32 [8192, 2048], P(('dp', 'tensor'))
- gains_grad: float32 [4, 2048], P(None, ('dp', 'tensor'))
- q_grad: float32 [2048, 2048], P('dp', 'tensor')
- k_grad: float32 [2048, 2048], P('dp', 'tensor')
- v_grad: float32 [2048, 2048], P('dp', 'tensor')
- o_grad: float32 [2048, 2048], P('tensor', 'dp')
- gate_grad: float32 [16, 2048, 1024], P(None, 'dp', 'tensor')
- up_grad: float32 [16, 2048, 1024], P(None, 'dp', 'tensor')
- down_grad: float32 [16, 1024, 2048], P(None, 'tensor', 'dp')
Inputs may be any that keep to these rules, and one draw needn't show every extreme that they name: `routes`: within each slot's 1024 tokens no expert is named by more than 768 tokens, a bound that some block reaches. The lengths sum to 7424 and the longest is exactly 1024.
All inputs are finite; a program needn't handle non-finite values. No bound on the sum of `lengths` on one device may be relied on, other than what follows from the above.
Results may differ from a plain program's by a relative error of at most 0.012.
Values may be sent and summed in bfloat16 or wider, within the bound.
A program may use at most 448 MiB of HBM per device.

v0:
```python
import math

import jax
import jax.numpy as jnp
from jax import lax
from jax.sharding import PartitionSpec as P

D = 2048
HEAD_DIM = 128
EXPERTS = 16
LEN = 1024


norm_eps = 1e-05


def rope_tables():
    half_width = HEAD_DIM // 2
    freqs = jnp.exp(-math.log(10000.0) * jnp.arange(half_width, dtype=jnp.float32) / half_width)
    angles = jnp.arange(LEN, dtype=jnp.float32)[:, None] * freqs[None, :]
    return (jnp.cos(angles), jnp.sin(angles))


def rotate(values, cosine_table, sine_table, direction):
    half_width = HEAD_DIM // 2
    front_half = values[..., :half_width]
    back_half = values[..., half_width:]
    cosine_part = cosine_table[None, :, None, :]
    sine_part = sine_table[None, :, None, :] * direction
    return jnp.concatenate(
        [
            front_half * cosine_part - back_half * sine_part,
            back_half * cosine_part + front_half * sine_part,
        ],
        axis=-1,
    )


def norm_rows(stream):
    scale = lax.rsqrt(jnp.mean(stream * stream, axis=1, keepdims=True) + norm_eps)
    return (stream * scale, scale)


def norm_back(d_normed, unit, scale, gain):
    weighted = d_normed * gain
    d_stream = scale * weighted - unit * (scale * jnp.mean(weighted * unit, axis=1, keepdims=True))
    return (d_stream, jnp.sum(d_normed * unit, axis=0))


def attention_scores(q_rot, k_rot, lengths):
    positions = jnp.arange(LEN, dtype=jnp.int32)
    allowed = (positions[None, None, :] <= positions[None, :, None]) & (
        positions[None, None, :] < lengths[:, None, None]
    )
    scores = jnp.einsum("sqhd,skhd->shqk", q_rot, k_rot, preferred_element_type=jnp.float32) * (
        1.0 / math.sqrt(HEAD_DIM)
    )
    return jnp.where(allowed[:, None], scores, -1e30)


def shards(
    hidden_in,
    norm_gains,
    q_weight,
    k_weight,
    v_weight,
    o_weight,
    gate_weight,
    up_weight,
    down_weight,
    lengths,
    routes,
    route_weights,
    out_grad,
):
    tensor_count = lax.axis_size("tensor")
    dp_count = lax.axis_size("dp")
    slots = lengths.shape[0]
    group_rows = slots * LEN
    own_rows = hidden_in.shape[0]
    width_local = q_weight.shape[1]
    heads_local = width_local // HEAD_DIM
    gain_width = norm_gains.shape[1]
    row_start = lax.axis_index("tensor") * own_rows
    col_start = lax.axis_index("tensor") * width_local
    cosine_table, sine_table = rope_tables()
    positions = jnp.arange(LEN, dtype=jnp.int32)
    valid_all = (positions[None, :] < lengths[:, None]).astype(jnp.float32).reshape(group_rows)
    valid_own = lax.dynamic_slice_in_dim(valid_all, row_start, own_rows)[:, None]
    gathered_x, gains_part = (
        lax.all_gather(hidden_in, "tensor", axis=0, tiled=True),
        lax.all_gather(norm_gains, "tensor", axis=1, tiled=True),
    )
    q_all, k_all, v_all, o_all, gate_all, up_all, down_all, gains_low = (
        lax.all_gather(q_weight, "dp", axis=0, tiled=True),
        lax.all_gather(k_weight, "dp", axis=0, tiled=True),
        lax.all_gather(v_weight, "dp", axis=0, tiled=True),
        lax.all_gather(o_weight, "dp", axis=1, tiled=True),
        lax.all_gather(gate_weight, "dp", axis=1, tiled=True),
        lax.all_gather(up_weight, "dp", axis=1, tiled=True),
        lax.all_gather(down_weight, "dp", axis=2, tiled=True),
        lax.all_gather(gains_part, "dp", axis=1, tiled=True),
    )
    gains = gains_low.astype(jnp.float32)
    gain_q = lax.dynamic_slice_in_dim(gains[1], col_start, width_local)
    gain_k = lax.dynamic_slice_in_dim(gains[2], col_start, width_local)
    unit1, scale1 = norm_rows(gathered_x.astype(jnp.float32))
    normed1 = (unit1 * gains[0]).astype(jnp.bfloat16)
    q_raw = jnp.dot(normed1, q_all, preferred_element_type=jnp.float32)
    k_raw = jnp.dot(normed1, k_all, preferred_element_type=jnp.float32)
    values = jnp.dot(normed1, v_all, preferred_element_type=jnp.float32).astype(jnp.bfloat16)
    q_squares, k_squares = lax.psum(
        (jnp.sum(q_raw * q_raw, axis=1), jnp.sum(k_raw * k_raw, axis=1)), "tensor"
    )
    q_scale = lax.rsqrt(q_squares / D + norm_eps)[:, None]
    k_scale = lax.rsqrt(k_squares / D + norm_eps)[:, None]
    q_unit = q_raw * q_scale
    k_unit = k_raw * k_scale
    head_shape = (slots, LEN, heads_local, HEAD_DIM)
    q_rot = rotate((q_unit * gain_q).reshape(head_shape), cosine_table, sine_table, 1.0).astype(
        jnp.bfloat16
    )
    k_rot = rotate((k_unit * gain_k).reshape(head_shape), cosine_table, sine_table, 1.0).astype(
        jnp.bfloat16
    )
    v_heads = values.reshape(head_shape)
    scores = attention_scores(q_rot, k_rot, lengths)
    row_max = jnp.max(scores, axis=-1, keepdims=True)
    log_total = row_max + jnp.log(jnp.sum(jnp.exp(scores - row_max), axis=-1, keepdims=True))
    probs = jnp.exp(scores - log_total).astype(jnp.bfloat16)
    attended = (
        jnp.einsum("shqk,skhd->sqhd", probs, v_heads, preferred_element_type=jnp.float32)
        .reshape(group_rows, width_local)
        .astype(jnp.bfloat16)
    )
    attn_terms = jnp.dot(attended, o_all, preferred_element_type=jnp.float32)
    branch = lax.psum_scatter(attn_terms, "tensor", scatter_dimension=0, tiled=True)
    mid_stream = hidden_in.astype(jnp.float32) + valid_own * branch
    mid_all = lax.all_gather(mid_stream, "tensor", axis=0, tiled=True)
    unit2, scale2 = norm_rows(mid_all)
    normed2 = (unit2 * gains[3]).astype(jnp.bfloat16)
    experts_all = jnp.arange(EXPERTS, dtype=jnp.int32)
    matches = (routes[:, :, None] == experts_all[None, None, :]).astype(jnp.float32)
    combine = jnp.sum(matches * route_weights[:, :, None], axis=1)
    weight_cols = jnp.transpose(combine)
    coef_cols = weight_cols * valid_all[None, :]

    def expert_forward(accum, expert_in):
        gate_mat, up_mat, down_mat, weight_col = expert_in
        gate_act = jnp.dot(normed2, gate_mat, preferred_element_type=jnp.float32)
        up_act = jnp.dot(normed2, up_mat, preferred_element_type=jnp.float32)
        inner_act = (jax.nn.silu(gate_act) * up_act).astype(jnp.bfloat16)
        expert_out = jnp.dot(inner_act, down_mat, preferred_element_type=jnp.float32)
        accum = accum + expert_out * weight_col[:, None]
        return (accum, (gate_act, up_act, inner_act))

    accum_start = jnp.zeros((group_rows, D), jnp.float32)
    moe_terms, kept_acts = lax.scan(
        expert_forward, accum_start, (gate_all, up_all, down_all, weight_cols)
    )
    mixed = lax.psum_scatter(moe_terms, "tensor", scatter_dimension=0, tiled=True)
    block_out = (mid_stream + valid_own * mixed).astype(jnp.bfloat16)
    cot_all = lax.all_gather(out_grad, "tensor", axis=0, tiled=True)
    gate_back, up_back, down_back = (gate_all, up_all, down_all)

    def expert_terms_of(accum, expert_in):
        gate_mat, up_mat, down_mat, coef_col, gate_act, up_act, inner_act = expert_in
        d_expert = (cot_all.astype(jnp.float32) * coef_col[:, None]).astype(jnp.bfloat16)
        grad_down = jnp.einsum("cf,cd->fd", inner_act, d_expert, preferred_element_type=jnp.float32)
        d_inner = jnp.einsum("cd,fd->cf", d_expert, down_mat, preferred_element_type=jnp.float32)
        sigmoid_val = jax.nn.sigmoid(gate_act)
        silu_val = gate_act * sigmoid_val
        d_gate = (d_inner * up_act * (sigmoid_val + silu_val * (1.0 - sigmoid_val))).astype(
            jnp.bfloat16
        )
        d_up = (d_inner * silu_val).astype(jnp.bfloat16)
        grad_gate = jnp.einsum("cd,cf->df", normed2, d_gate, preferred_element_type=jnp.float32)
        grad_up = jnp.einsum("cd,cf->df", normed2, d_up, preferred_element_type=jnp.float32)
        d_picked = jnp.einsum(
            "cf,df->cd", d_gate, gate_mat, preferred_element_type=jnp.float32
        ) + jnp.einsum("cf,df->cd", d_up, up_mat, preferred_element_type=jnp.float32)
        accum = accum + d_picked
        return (accum, (grad_gate, grad_up, grad_down))

    backward_in = (gate_back, up_back, down_back, coef_cols) + kept_acts
    d_normed2, expert_terms = lax.scan(expert_terms_of, accum_start, backward_in)
    gate_grad, up_grad, down_grad = (
        lax.psum_scatter(expert_terms[0], "dp", scatter_dimension=1, tiled=True),
        lax.psum_scatter(expert_terms[1], "dp", scatter_dimension=1, tiled=True),
        lax.psum_scatter(expert_terms[2], "dp", scatter_dimension=2, tiled=True),
    )
    d_mid_terms, gain2_term = norm_back(d_normed2, unit2, scale2, gains[3])
    d_mid = out_grad.astype(jnp.float32) + lax.psum_scatter(
        d_mid_terms, "tensor", scatter_dimension=0, tiled=True
    )
    d_branch = (valid_own * d_mid).astype(jnp.bfloat16)
    d_branch_all = lax.all_gather(d_branch, "tensor", axis=0, tiled=True)
    o_term = jnp.einsum("rw,rd->wd", attended, d_branch_all, preferred_element_type=jnp.float32)
    d_attended = (
        jnp.einsum("rd,wd->rw", d_branch_all, o_all, preferred_element_type=jnp.float32)
        .astype(jnp.bfloat16)
        .reshape(head_shape)
    )
    probs_full = jnp.exp(attention_scores(q_rot, k_rot, lengths) - log_total)
    d_values = jnp.einsum(
        "shqk,sqhd->skhd",
        probs_full.astype(jnp.bfloat16),
        d_attended,
        preferred_element_type=jnp.float32,
    ).astype(jnp.bfloat16)
    d_probs = jnp.einsum("sqhd,skhd->shqk", d_attended, v_heads, preferred_element_type=jnp.float32)
    d_scores = (
        probs_full * (d_probs - jnp.sum(probs_full * d_probs, axis=-1, keepdims=True))
    ).astype(jnp.bfloat16)
    score_scale = 1.0 / math.sqrt(HEAD_DIM)
    d_qrot = (
        jnp.einsum("shqk,skhd->sqhd", d_scores, k_rot, preferred_element_type=jnp.float32)
        * score_scale
    )
    d_krot = (
        jnp.einsum("shqk,sqhd->skhd", d_scores, q_rot, preferred_element_type=jnp.float32)
        * score_scale
    )
    d_qn = rotate(d_qrot, cosine_table, sine_table, -1.0).reshape(group_rows, width_local)
    d_kn = rotate(d_krot, cosine_table, sine_table, -1.0).reshape(group_rows, width_local)
    q_weighted = d_qn * gain_q
    k_weighted = d_kn * gain_k
    q_total, k_total = lax.psum(
        (jnp.sum(q_weighted * q_unit, axis=1), jnp.sum(k_weighted * k_unit, axis=1)), "tensor"
    )
    d_q = (q_scale * q_weighted - q_unit * (q_scale * (q_total / D)[:, None])).astype(jnp.bfloat16)
    d_k = (k_scale * k_weighted - k_unit * (k_scale * (k_total / D)[:, None])).astype(jnp.bfloat16)
    d_v = d_values.reshape(group_rows, width_local)
    q_term = jnp.einsum("rd,rw->dw", normed1, d_q, preferred_element_type=jnp.float32)
    k_term = jnp.einsum("rd,rw->dw", normed1, d_k, preferred_element_type=jnp.float32)
    v_term = jnp.einsum("rd,rw->dw", normed1, d_v, preferred_element_type=jnp.float32)
    d_normed1 = (
        jnp.einsum("rw,dw->rd", d_q, q_all, preferred_element_type=jnp.float32)
        + jnp.einsum("rw,dw->rd", d_k, k_all, preferred_element_type=jnp.float32)
        + jnp.einsum("rw,dw->rd", d_v, v_all, preferred_element_type=jnp.float32)
    )
    d_input_terms, gain1_term = norm_back(d_normed1, unit1, scale1, gains[0])
    zero_row = jnp.zeros((D,), jnp.float32)
    gainq_term = lax.dynamic_update_slice_in_dim(
        zero_row, jnp.sum(d_qn * q_unit, axis=0), col_start, 0
    )
    gaink_term = lax.dynamic_update_slice_in_dim(
        zero_row, jnp.sum(d_kn * k_unit, axis=0), col_start, 0
    )
    gain_terms = jnp.stack([gain1_term, gainq_term, gaink_term, gain2_term], axis=0)
    arranged = (
        gain_terms.reshape(4, dp_count, tensor_count, gain_width)
        .transpose(2, 0, 1, 3)
        .reshape(tensor_count, 4 * dp_count * gain_width)
    )
    d_input_own, gains_piece = (
        lax.psum_scatter(d_input_terms, "tensor", scatter_dimension=0, tiled=True),
        lax.psum_scatter(arranged, "tensor", scatter_dimension=0, tiled=True),
    )
    input_grad = d_mid + d_input_own
    gains_piece = gains_piece.reshape(4, dp_count * gain_width)
    q_grad, k_grad, v_grad, o_grad, gains_grad = (
        lax.psum_scatter(q_term, "dp", scatter_dimension=0, tiled=True),
        lax.psum_scatter(k_term, "dp", scatter_dimension=0, tiled=True),
        lax.psum_scatter(v_term, "dp", scatter_dimension=0, tiled=True),
        lax.psum_scatter(o_term, "dp", scatter_dimension=1, tiled=True),
        lax.psum_scatter(gains_piece, "dp", scatter_dimension=1, tiled=True),
    )
    return (
        block_out,
        input_grad,
        gains_grad,
        q_grad,
        k_grad,
        v_grad,
        o_grad,
        gate_grad,
        up_grad,
        down_grad,
    )


def solution(mesh):
    placed = (
        P(("dp", "tensor"), None),
        P(None, ("dp", "tensor")),
        P("dp", "tensor"),
        P("dp", "tensor"),
        P("dp", "tensor"),
        P("tensor", "dp"),
        P(None, "dp", "tensor"),
        P(None, "dp", "tensor"),
        P(None, "tensor", "dp"),
        P("dp"),
        P("dp", None),
        P("dp", None),
        P(("dp", "tensor"), None),
    )
    return jax.shard_map(
        shards,
        mesh=mesh,
        in_specs=placed,
        out_specs=(
            P(("dp", "tensor"), None),
            P(("dp", "tensor"), None),
            P(None, ("dp", "tensor")),
            P("dp", "tensor"),
            P("dp", "tensor"),
            P("dp", "tensor"),
            P("tensor", "dp"),
            P(None, "dp", "tensor"),
            P(None, "dp", "tensor"),
            P(None, "tensor", "dp"),
        ),
        check_vma=False,
    )
```

profile of v0, /device:TPU:0, one launch (start us, length us, event | category | flops | bytes accessed | tf_op | source)
XLA Modules:
  0.0 3074.1 jit_solution(11654959885005497005)
XLA Ops:
  11.3 12.9 all-gather
  36.6 56.4 %all-gather.13.cloned.1.call-done = bf16[1024,2048]{1,0:T(8,128)(2,1)} async-done(((bf16[256,2048]{1,0:T(8,128)(2,1)}), bf16[1024,2048]{1,0:T(8,128)(2,1)}) %all-gather.13.cloned.1.call-update) | async-done | bytes 4194320 | tf_op jit(solution)/shard_map/all_gather | solution.py:91
  96.2 25.1 all-gather.17.cloned.1.call-done
  127.9 23.0 all-gather.19.cloned.1.call-done
  225.5 142.1 %reduce-scatter.15.cloned.1.call-done = f32[256,2048]{1,0:T(8,128)} async-done(((f32[1024,2048]{1,0:T(8,128)}), f32[256,2048]{1,0:T(8,128)}) %reduce-scatter.15.cloned.1.call-update) | async-done | bytes 2097168 | tf_op jit(solution)/shard_map/reduce_scatter | solution.py:137
  373.8 147.3 %all-gather.25.cloned.1.call-done = f32[1024,2048]{1,0:T(8,128)} async-done(((f32[256,2048]{1,0:T(8,128)}), f32[1024,2048]{1,0:T(8,128)}) %all-gather.25.cloned.1.call-update) | async-done | bytes 8388624 | tf_op jit(solution)/shard_map/all_gather | solution.py:139
  529.9 81.1 %all-gather.23.cloned.1.call-done = bf16[16,2048,256]{2,1,0:T(8,128)(2,1)} async-done(((bf16[16,256,256]{2,1,0:T(8,128)(2,1)}), bf16[16,2048,256]{2,1,0:T(8,128)(2,1)}) %all-gather.23.cloned.1.call-update) | async-done | bytes 16777232 | tf_op jit(solution)/shard_map/all_gather | solution.py:99
  611.0 91.7 %all-gather.27.cloned.1.call-done = bf16[16,2048,256]{2,1,0:T(8,128)(2,1)} async-done(((bf16[16,256,256]{2,1,0:T(8,128)(2,1)}), bf16[16,2048,256]{2,1,0:T(8,128)(2,1)}) %all-gather.27.cloned.1.call-update) | async-done | bytes 16777232 | tf_op jit(solution)/shard_map/all_gather | solution.py:100
  702.7 94.8 %all-gather.29.cloned.1.call-done = bf16[16,256,2048]{2,1,0:T(8,128)(2,1)} async-done(((bf16[16,256,256]{2,1,0:T(8,128)(2,1)}), bf16[16,256,2048]{2,1,0:T(8,128)(2,1)}) %all-gather.29.cloned.1.call-update) | async-done | bytes 16777232 | tf_op jit(solution)/shard_map/all_gather | solution.py:101
  797.4 260.3 %while.34 = (s32[]{:T(128)}, f32[1024,2048]{1,0:T(8,128)}, f32[16,1024,256]{1,2,0:T(8,128)}, f32[16,1024,256]{1,2,0:T(8,128)}, bf16[16,1024,256]{1,2,0:T(8,128)(...) while((s32[]{:T(128)}, f32[1024,2048]{1,0:T(8,128)}, ...), condition=%wide.region_11.12_spmd.clone, body=%wide.region_10.11_spmd.clone.sunk | while | flops 3229089792 | bytes 111687928 | solution.py:158
  1057.8 614.1 %while.35 = (s32[]{:T(128)}, f32[1024,2048]{1,0:T(8,128)}, f32[16,2048,256]{2,1,0:T(8,128)}, f32[16,2048,256]{2,1,0:T(8,128)}, f32[16,256,2048]{2,1,0:T(8,128)},...) while((s32[]{:T(128)}, f32[1024,2048]{1,0:T(8,128)}, ...), condition=%wide.region_14.15_spmd.clone, body=%wide.region_13.14_spmd.clone.sunk | while | flops 6464471040 | bytes 138954096 | solution.py:186
  1686.9 144.3 %reduce-scatter.19.cloned.1.call-done = f32[256,2048]{1,0:T(8,128)} async-done(((f32[1024,2048]{1,0:T(8,128)}), f32[256,2048]{1,0:T(8,128)}) %reduce-scatter.19.cloned.1.call-update) | async-done | bytes 2097168 | tf_op jit(solution)/shard_map/reduce_scatter | solution.py:193
  1836.7 80.6 %all-gather.33.cloned.1.call-done = bf16[1024,2048]{1,0:T(8,128)(2,1)} async-done(((bf16[256,2048]{1,0:T(8,128)(2,1)}), bf16[1024,2048]{1,0:T(8,128)(2,1)}) %all-gather.33.cloned.1.call-update) | async-done | bytes 4194320 | tf_op jit(solution)/shard_map/all_gather | solution.py:197
  1932.1 12.6 multiply_reduce_fusion
  1944.7 13.1 multiply_convert_fusion.4
  2020.3 17.1 all-reduce
  2081.2 136.8 %reduce-scatter.21.cloned.1.call-done = f32[256,2048]{1,0:T(8,128)} async-done(((f32[1024,2048]{1,0:T(8,128)}), f32[256,2048]{1,0:T(8,128)}) %reduce-scatter.21.cloned.1.call-update) | async-done | bytes 2097168 | tf_op jit(solution)/shard_map/reduce_scatter | solution.py:257
  2221.3 52.2 %reduce-scatter.29.cloned.1.call-done = f32[512,256]{1,0:T(8,128)} async-done(((f32[512,2048]{1,0:T(8,128)}), f32[512,256]{1,0:T(8,128)}) %reduce-scatter.29.cloned.1.call-update) | async-done | bytes 524304 | tf_op jit(solution)/shard_map/reduce_scatter | solution.py:266
  2273.5 55.0 %reduce-scatter.27.cloned.1.call-done = f32[256,512]{1,0:T(8,128)} async-done(((f32[2048,512]{1,0:T(8,128)}), f32[256,512]{1,0:T(8,128)}) %reduce-scatter.27.cloned.1.call-update) | async-done | bytes 524304 | tf_op jit(solution)/shard_map/reduce_scatter | solution.py:265
  2328.5 55.1 %reduce-scatter.25.cloned.1.call-done = f32[256,512]{1,0:T(8,128)} async-done(((f32[2048,512]{1,0:T(8,128)}), f32[256,512]{1,0:T(8,128)}) %reduce-scatter.25.cloned.1.call-update) | async-done | bytes 524304 | tf_op jit(solution)/shard_map/reduce_scatter | solution.py:264
  2383.6 55.0 %reduce-scatter.23.cloned.1.call-done = f32[256,512]{1,0:T(8,128)} async-done(((f32[2048,512]{1,0:T(8,128)}), f32[256,512]{1,0:T(8,128)}) %reduce-scatter.23.cloned.1.call-update) | async-done | bytes 524304 | tf_op jit(solution)/shard_map/reduce_scatter | solution.py:263
  2438.5 209.5 %reduce-scatter.35.cloned.1.call-done = f32[16,256,256]{2,1,0:T(8,128)} async-done(((f32[16,256,2048]{2,1,0:T(8,128)}), f32[16,256,256]{2,1,0:T(8,128)}) %reduce-scatter.35.cloned.1.call-update) | async-done | bytes 4194320 | tf_op jit(solution)/shard_map/reduce_scatter | solution.py:190
  2648.0 209.6 %reduce-scatter.31.cloned.1.call-done = f32[16,256,256]{2,1,0:T(8,128)} async-done(((f32[16,2048,256]{2,1,0:T(8,128)}), f32[16,256,256]{2,1,0:T(8,128)}) %reduce-scatter.31.cloned.1.call-update) | async-done | bytes 4194320 | tf_op jit(solution)/shard_map/reduce_scatter | solution.py:188
  2857.6 209.7 %reduce-scatter.33.cloned.1.call-done = f32[16,256,256]{2,1,0:T(8,128)} async-done(((f32[16,2048,256]{2,1,0:T(8,128)}), f32[16,256,256]{2,1,0:T(8,128)}) %reduce-scatter.33.cloned.1.call-update) | async-done | bytes 4194320 | tf_op jit(solution)/shard_map/reduce_scatter | solution.py:189
  (920 shorter events, 1131.4 us)
Async XLA Ops:
  7.2 85.9 %all-gather.13.cloned.1.call-start = ((), (), s32[]{:S(2)}) async-start(), calls=%async_computation.12 | async-start | bytes 5242880 | tf_op jit(solution)/shard_map/all_gather | solution.py:91
  7.9 113.3 %all-gather.17.cloned.1.call-start = ((), (), s32[]{:S(2)}) async-start(), calls=%async_computation.14 | async-start | bytes 2359296 | tf_op jit(solution)/shard_map/all_gather | solution.py:95
  8.7 142.3 %all-gather.19.cloned.1.call-start = ((), (), s32[]{:S(2)}) async-start(), calls=%async_computation.15 | async-start | bytes 2359296 | tf_op jit(solution)/shard_map/all_gather | solution.py:96
  9.4 194.8 %all-gather.15.cloned.1.call-start = ((), (), s32[]{:S(2)}) async-start(), calls=%async_computation.13 | async-start | bytes 2359296 | tf_op jit(solution)/shard_map/all_gather | solution.py:97
  10.0 207.7 %all-gather.21.cloned.1.call-start = ((), (), s32[]{:S(2)}) async-start(), calls=%async_computation.16 | async-start | bytes 2359296 | tf_op jit(solution)/shard_map/all_gather | solution.py:98
  10.6 357.0 %reduce-scatter.15.cloned.1.call-start = ((), (), s32[]{:S(2)}) async-start(), calls=%async_computation.17 | async-start | bytes 10485760 | tf_op jit(solution)/shard_map/reduce_scatter | solution.py:137
  225.4 295.8 %all-gather.25.cloned.1.call-start = ((), (), s32[]{:S(2)}) async-start(), calls=%async_computation.19 | async-start | bytes 10485760 | tf_op jit(solution)/shard_map/all_gather | solution.py:139
  370.8 240.2 %all-gather.23.cloned.1.call-start = ((), (), s32[]{:S(2)}) async-start(), calls=%async_computation.18 | async-start | bytes 18874368 | tf_op jit(solution)/shard_map/all_gather | solution.py:99
  371.6 331.1 %all-gather.27.cloned.1.call-start = ((), (), s32[]{:S(2)}) async-start(), calls=%async_computation.20 | async-start | bytes 18874368 | tf_op jit(solution)/shard_map/all_gather | solution.py:100
  372.3 425.2 %all-gather.29.cloned.1.call-start = ((), (), s32[]{:S(2)}) async-start(), calls=%async_computation.21 | async-start | bytes 18874368 | tf_op jit(solution)/shard_map/all_gather | solution.py:101
  372.9 684.9 %all-gather.31.cloned.1.call-start = ((), (), s32[]{:S(2)}) async-start(), calls=%async_computation.23 | async-start | bytes 5242880 | tf_op jit(solution)/shard_map/all_gather | solution.py:163
  373.6 1313.3 %reduce-scatter.17.cloned.1.call-start = ((), (), s32[]{:S(2)}) async-start(), calls=%async_computation.22 | async-start | bytes 10485760 | tf_op jit(solution)/shard_map/reduce_scatter | solution.py:161
  1057.7 773.5 %reduce-scatter.19.cloned.1.call-start = ((), (), s32[]{:S(2)}) async-start(), calls=%async_computation.24 | async-start | bytes 10485760 | tf_op jit(solution)/shard_map/reduce_scatter | solution.py:193
  1057.8 614.2 %copy-start.41 = (f32[1,2048]{1,0:T(1,128)S(1)}, f32[1,2048]{1,0:T(1,128)}, u32[]{:S(2)}) copy-start(f32[1,2048]{1,0:T(1,128)} %copy-done.40) | copy-start | bytes 24580
  1686.9 230.4 %all-gather.33.cloned.1.call-start = ((), (), s32[]{:S(2)}) async-start(), calls=%async_computation.25 | async-start | bytes 5242880 | tf_op jit(solution)/shard_map/all_gather | solution.py:197
  1835.7 243.5 %reduce-scatter.37.cloned.1.call-start = ((), (), s32[]{:S(2)}) async-start(), calls=%async_computation.34 | async-start | bytes 294912
  2038.9 179.0 %reduce-scatter.21.cloned.1.call-start = ((), (), s32[]{:S(2)}) async-start(), calls=%async_computation.26 | async-start | bytes 10485760 | tf_op jit(solution)/shard_map/reduce_scatter | solution.py:257
  2046.6 226.8 %reduce-scatter.29.cloned.1.call-start = ((), (), s32[]{:S(2)}) async-start(), calls=%async_computation.30 | async-start | bytes 4718592 | tf_op jit(solution)/shard_map/reduce_scatter | solution.py:266
  2053.6 274.9 %reduce-scatter.27.cloned.1.call-start = ((), (), s32[]{:S(2)}) async-start(), calls=%async_computation.29 | async-start | bytes 4718592 | tf_op jit(solution)/shard_map/reduce_scatter | solution.py:265
  2060.9 322.7 %reduce-scatter.25.cloned.1.call-start = ((), (), s32[]{:S(2)}) async-start(), calls=%async_computation.28 | async-start | bytes 4718592 | tf_op jit(solution)/shard_map/reduce_scatter | solution.py:264
  2068.9 369.6 %reduce-scatter.23.cloned.1.call-start = ((), (), s32[]{:S(2)}) async-start(), calls=%async_computation.27 | async-start | bytes 4718592 | tf_op jit(solution)/shard_map/reduce_scatter | solution.py:263
  2077.0 571.0 %reduce-scatter.35.cloned.1.call-start = ((), (), s32[]{:S(2)}) async-start(), calls=%async_computation.33 | async-start | bytes 37748736 | tf_op jit(solution)/shard_map/reduce_scatter | solution.py:190
  2077.8 779.9 %reduce-scatter.31.cloned.1.call-start = ((), (), s32[]{:S(2)}) async-start(), calls=%async_computation.31 | async-start | bytes 37748736 | tf_op jit(solution)/shard_map/reduce_scatter | solution.py:188
  2078.5 988.8 %reduce-scatter.33.cloned.1.call-start = ((), (), s32[]{:S(2)}) async-start(), calls=%async_computation.32 | async-start | bytes 37748736 | tf_op jit(solution)/shard_map/reduce_scatter | solution.py:189
  (225 other events, 4197.9 us)
Sparse Core Ops, SparseCore 0:
  9.6 83.4 all-gather.12
  94.9 26.2 all-gather.16
  123.1 27.7 all-gather.18
  152.7 27.7 all-gather.14
  182.2 28.0 all-gather.20
  225.5 141.9 reduce-scatter.14
  370.9 150.2 all-gather.24
  523.0 87.9 all-gather.22
  612.9 89.7 all-gather.26
  704.4 93.0 all-gather.28
  799.0 80.7 all-gather.30
  1057.9 144.4 reduce-scatter.16
  1687.0 144.2 reduce-scatter.18
  1835.8 81.3 all-gather.32
  2039.1 31.9 reduce-scatter.36
  2073.3 144.5 reduce-scatter.20
  2221.7 51.7 reduce-scatter.28
  2277.3 51.1 reduce-scatter.26
  2332.4 51.1 reduce-scatter.24
  2387.4 51.1 reduce-scatter.22
  2442.7 205.2 reduce-scatter.34
  2652.1 205.4 reduce-scatter.30
  2861.8 205.4 reduce-scatter.32
where the time goes:
time: 3080 us; the launch traced here: 3070 us
  waiting for transfers between devices  1880 us (61%)
  matrix products  753 us (24%)
  local copies, waits for them, and re-layouts  276 us (9%)
  other arithmetic  89 us (3%)
  blocking collectives  60.3 us (2%)
    reduce_scatter x1, waiting for transfers between devices, shards(): lax.psum_scatter(expert_terms[1], 'dp', scatter_dimension=1, tiled=True)  210 us
    reduce_scatter x1, waiting for transfers between devices, shards(): lax.psum_scatter(expert_terms[0], 'dp', scatter_dimension=1, tiled=True)  210 us
    reduce_scatter x1, waiting for transfers between devices, shards(): lax.psum_scatter(expert_terms[2], 'dp', scatter_dimension=2, tiled=True)  209 us
    all_gather x1, waiting for transfers between devices, shards(): mid_all = lax.all_gather(mid_stream, 'tensor', axis=0, tiled=True)  147 us
    reduce_scatter x1, waiting for transfers between devices, shards(): lax.psum_scatter(d_mid_terms, 'tensor', scatter_dimension=0, tiled=True)  144 us
    reduce_scatter x1, waiting for transfers between devices, shards(): lax.psum_scatter(attn_terms, 'tensor', scatter_dimension=0, tiled=True)  142 us
    reduce_scatter x1, waiting for transfers between devices, shards(): lax.psum_scatter(d_input_terms, 'tensor', scatter_dimension=0, tiled=True)  137 us
    dot_general x16, matrix products, expert_terms_of(): jnp.einsum('cf,df->cd', d_up, up_mat, preferred_element_type=jnp.float32)  134 us
  transfers between devices with their start and end apart: 23, of which 18 were waited for; matrix products, arithmetic and copies ran while one was open for 31% of the time, Pallas kernels for 0%

commit v1 on v0

v1 whole, which is shorter than its diff:
```python
import functools
import math

import jax
import jax.numpy as jnp
from jax import lax
from jax.experimental import pallas as pl
from jax.experimental.pallas import tpu as pltpu
from jax.sharding import PartitionSpec as P

D = 2048
HEAD_DIM = 128
EXPERTS = 16
LEN = 1024

norm_eps = 1e-05
BF = jnp.bfloat16
F32 = jnp.float32
SCALE = 1.0 / math.sqrt(HEAD_DIM)
NEG = -1e30
VMEM_LIMIT = 60 * 1024 * 1024


def rope_tables():
    half_width = HEAD_DIM // 2
    freqs = jnp.exp(-math.log(10000.0) * jnp.arange(half_width, dtype=F32) / half_width)
    angles = jnp.arange(LEN, dtype=F32)[:, None] * freqs[None, :]
    cosine, sine = jnp.cos(angles), jnp.sin(angles)
    return (
        jnp.concatenate([cosine, cosine], axis=1),
        jnp.concatenate([-sine, sine], axis=1),
    )


def norm_rows(stream):
    scale = lax.rsqrt(jnp.mean(stream * stream, axis=1, keepdims=True) + norm_eps)
    return (stream * scale, scale)


def norm_back(d_normed, unit, scale, gain):
    weighted = d_normed * gain
    return scale * weighted - unit * (scale * jnp.mean(weighted * unit, axis=1, keepdims=True))


def dot_nt(left, right):
    return lax.dot_general(left, right, (((1,), (1,)), ((), ())), preferred_element_type=F32)


def dot_tn(left, right):
    return lax.dot_general(left, right, (((0,), (0,)), ((), ())), preferred_element_type=F32)


def dot(left, right):
    return jnp.dot(left, right, preferred_element_type=F32)


def line_gather(own, count, me):
    rows = own.shape[0]
    rightward = [(i, i + 1) for i in range(count - 1)]
    leftward = [(i + 1, i) for i in range(count - 1)]
    from_left, from_right = [own], [own]
    for step in range(1, count):
        from_left.append(lax.ppermute(from_left[-1], "tensor", rightward[step - 1 :]))
        from_right.append(lax.ppermute(from_right[-1], "tensor", leftward[: count - step]))
    out = jnp.zeros((count * rows,) + own.shape[1:], own.dtype)
    out = lax.dynamic_update_slice_in_dim(out, own, me * rows, 0)
    for step in range(1, count):
        block = jnp.where(me >= step, from_left[step], from_right[count - step])
        out = lax.dynamic_update_slice_in_dim(out, block, lax.rem(me - step + count, count) * rows, 0)
    return out


def line_reduce(partial, count, me):
    rows = partial.shape[0] // count

    def block(index):
        return lax.dynamic_slice_in_dim(partial, lax.rem(index + count, count) * rows, rows, 0)

    left, right = None, None
    for step in range(1, count):
        rightward = [(i, i + 1) for i in range(step)]
        leftward = [(count - 1 - i, count - 2 - i) for i in range(step)]
        to_right, to_left = block(me - step), block(me + step)
        if left is not None:
            to_right = (to_right.astype(F32) + left.astype(F32)).astype(BF)
            to_left = (to_left.astype(F32) + right.astype(F32)).astype(BF)
        left = lax.ppermute(to_right, "tensor", rightward)
        right = lax.ppermute(to_left, "tensor", leftward)
    return block(me).astype(F32) + left.astype(F32) + right.astype(F32)


def small_kernel(axis, count, mode, x_ref, out_ref, held, send_sems, recv_sems):
    me = lax.axis_index(axis)
    barrier = pltpu.get_barrier_semaphore()
    for shift in range(1, count):
        peer = lax.rem(me + shift, count)
        pl.semaphore_signal(barrier, inc=1, device_id={axis: peer}, device_id_type=pl.DeviceIdType.MESH)
    pl.semaphore_wait(barrier, count - 1)
    copies = []
    for shift in range(1, count):
        peer = lax.rem(me + shift, count)
        copies.append(
            pltpu.make_async_remote_copy(
                src_ref=x_ref.at[peer] if mode == "scatter" else x_ref,
                dst_ref=held.at[me],
                send_sem=send_sems.at[shift],
                recv_sem=recv_sems.at[shift],
                device_id={axis: peer},
                device_id_type=pl.DeviceIdType.MESH,
            )
        )
        copies[-1].start()
    held[me] = x_ref[me] if mode == "scatter" else x_ref[...]
    for copy in copies:
        copy.wait()
    if mode == "gather":
        out_ref[...] = held[...]
    else:
        total = held[0]
        for index in range(1, count):
            total = total + held[index]
        out_ref[...] = total


def small_exchange(x, axis, mode, collective_id):
    count = lax.axis_size(axis)
    piece = x.shape[1:] if mode == "scatter" else x.shape
    out_shape = (count,) + piece if mode == "gather" else piece
    return pl.pallas_call(
        functools.partial(small_kernel, axis, count, mode),
        in_specs=[pl.BlockSpec(memory_space=pltpu.VMEM)],
        out_specs=pl.BlockSpec(memory_space=pltpu.VMEM),
        out_shape=jax.ShapeDtypeStruct(out_shape, F32),
        scratch_shapes=[
            pltpu.VMEM((count,) + piece, F32),
            pltpu.SemaphoreType.DMA((count,)),
            pltpu.SemaphoreType.DMA((count,)),
        ],
        compiler_params=pltpu.CompilerParams(collective_id=collective_id, has_side_effects=True),
        name=f"small_{mode}_{collective_id}",
    )(x)


def flip(x, count, bit):
    return lax.ppermute(x, "dp", [(i, i ^ (1 << bit)) for i in range(count)])


def cube_gather(parts, count):
    bits = list(range(1, count.bit_length() - 1))
    orders = (bits, bits[::-1])
    held = []
    for part, order in zip(parts, orders):
        blocks = {0: part}
        for bit in order:
            keys = sorted(blocks)
            got = flip(jnp.stack([blocks[k] for k in keys]), count, bit)
            for n, k in enumerate(keys):
                blocks[k ^ (1 << bit)] = got[n]
        keys = sorted(blocks)
        got = flip(jnp.stack([blocks[k] for k in keys]), count, 0)
        for n, k in enumerate(keys):
            blocks[k ^ 1] = got[n]
        held.append(blocks)
    return held


def cube_pair(keep, away, count):
    return (keep.astype(F32) + flip(away, count, 0).astype(F32)).astype(BF)


def cube_step(parts, count, turn):
    bits = list(range(count.bit_length() - 2))
    out = []
    for blocks, order in zip(parts, (bits, bits[::-1])):
        mask = 1 << order[turn]
        sent = sorted(i for i in blocks if i & mask)
        got = flip(jnp.stack([blocks[i] for i in sent]), count, order[turn] + 1)
        kind = F32 if turn == len(order) - 1 else BF
        out.append(
            {i ^ mask: (blocks[i ^ mask].astype(F32) + got[k].astype(F32)).astype(kind) for k, i in enumerate(sent)}
        )
    return out


def cube_parts(total):
    middle = total.shape[1] // 2
    return [{i: part[i] for i in range(total.shape[0])} for part in (total[:, :middle], total[:, middle:])]


def cube_rest(parts, count, start=0):
    for turn in range(start, count.bit_length() - 2):
        parts = cube_step(parts, count, turn)
    return jnp.concatenate([blocks[0] for blocks in parts], axis=0)


def rotated(values, cosine, sine):
    return values * cosine + pltpu.roll(values, HEAD_DIM // 2, 1) * sine


def rotated_back(values, cosine, sine):
    return values * cosine - pltpu.roll(values, HEAD_DIM // 2, 1) * sine


QBLOCK = 256


def score_mask(row0, extent, length):
    row = lax.broadcasted_iota(jnp.int32, (QBLOCK, extent), 0) + row0
    col = lax.broadcasted_iota(jnp.int32, (QBLOCK, extent), 1)
    return (col <= row) & (col < length)


def attn_fwd_kernel(
    len_ref, q_ref, k_ref, v_ref, qs_ref, ks_ref, gq_ref, gk_ref, cos_ref, sin_ref,
    att_ref, qr_ref, kr_ref, lse_ref,
):
    length = len_ref[0]
    cosine, sine = cos_ref[...], sin_ref[...]
    qr_ref[...] = rotated(q_ref[...] * qs_ref[...] * gq_ref[...], cosine, sine).astype(BF)
    kr_ref[...] = rotated(k_ref[...] * ks_ref[...] * gk_ref[...], cosine, sine).astype(BF)
    for i in range(LEN // QBLOCK):
        extent = (i + 1) * QBLOCK
        rows = slice(i * QBLOCK, extent)
        scores = dot_nt(qr_ref[rows, :], kr_ref[:extent, :]) * SCALE
        scores = jnp.where(score_mask(i * QBLOCK, extent, length), scores, NEG)
        top = jnp.max(scores, axis=1, keepdims=True)
        weights = jnp.exp(scores - top)
        total = jnp.sum(weights, axis=1, keepdims=True)
        probs = (weights * (1.0 / total)).astype(BF)
        att_ref[rows, :] = dot(probs, v_ref[:extent, :]).astype(BF)
        lse_ref[0, rows, :] = top + jnp.log(total)


def column_spec(width=HEAD_DIM):
    return pl.BlockSpec((LEN, width), lambda h, *_: (0, h))


def whole_spec(shape):
    return pl.BlockSpec(shape, lambda h, *_: (0,) * len(shape))


def attention_forward(lengths, q_raw, k_raw, values, q_scale, k_scale, gain_q, gain_k, cosine, sine):
    width = q_raw.shape[1]
    heads = width // HEAD_DIM
    gain_spec = pl.BlockSpec((1, HEAD_DIM), lambda h, *_: (0, h))
    return pl.pallas_call(
        attn_fwd_kernel,
        grid_spec=pltpu.PrefetchScalarGridSpec(
            num_scalar_prefetch=1,
            grid=(heads,),
            in_specs=[column_spec()] * 3
            + [whole_spec((LEN, 1))] * 2
            + [gain_spec] * 2
            + [whole_spec((LEN, HEAD_DIM))] * 2,
            out_specs=[column_spec()] * 3 + [pl.BlockSpec((1, LEN, 1), lambda h, *_: (h, 0, 0))],
        ),
        out_shape=[jax.ShapeDtypeStruct((LEN, width), BF)] * 3
        + [jax.ShapeDtypeStruct((heads, LEN, 1), F32)],
        compiler_params=pltpu.CompilerParams(vmem_limit_bytes=VMEM_LIMIT),
        cost_estimate=pl.CostEstimate(
            flops=4 * LEN * LEN * width, bytes_accessed=16 * LEN * width, transcendentals=heads * LEN * LEN
        ),
        name="attn_fwd",
    )(lengths, q_raw, k_raw, values, q_scale, k_scale, gain_q, gain_k, cosine, sine)


def attn_bwd_kernel(
    len_ref, qr_ref, kr_ref, v_ref, da_ref, lse_ref, q_ref, k_ref, qs_ref, ks_ref, gq_ref, gk_ref, cos_ref, sin_ref,
    dqn_ref, dkn_ref, dv_ref, qsum_ref, ksum_ref, gqg_ref, gkg_ref,
    dk_acc, dv_acc, dq_acc,
):
    length = len_ref[0]
    head = pl.program_id(0)
    dk_acc[...] = jnp.zeros_like(dk_acc)
    dv_acc[...] = jnp.zeros_like(dv_acc)
    for i in range(LEN // QBLOCK):
        extent = (i + 1) * QBLOCK
        rows = slice(i * QBLOCK, extent)
        q_block, k_all, da = qr_ref[rows, :], kr_ref[:extent, :], da_ref[rows, :]
        scores = dot_nt(q_block, k_all) * SCALE
        mask = score_mask(i * QBLOCK, extent, length)
        full = jnp.exp(jnp.where(mask, scores, NEG) - lse_ref[0, rows, :])
        d_probs = dot_nt(da, v_ref[:extent, :])
        inner = jnp.sum(full * d_probs, axis=1, keepdims=True)
        d_scores = (full * (d_probs - inner)).astype(BF)
        dv_acc[:extent, :] += dot_tn(full.astype(BF), da)
        dk_acc[:extent, :] += dot_tn(d_scores, q_block)
        dq_acc[rows, :] = dot(d_scores, k_all)
    cosine, sine = cos_ref[...], sin_ref[...]
    dv_ref[...] = dv_acc[...].astype(BF)
    d_qn = rotated_back(dq_acc[...] * SCALE, cosine, sine)
    d_kn = rotated_back(dk_acc[...] * SCALE, cosine, sine)
    dqn_ref[...] = d_qn
    dkn_ref[...] = d_kn
    q_terms = d_qn * (q_ref[...] * qs_ref[...])
    k_terms = d_kn * (k_ref[...] * ks_ref[...])
    gqg_ref[...] = jnp.sum(q_terms, axis=0, keepdims=True)
    gkg_ref[...] = jnp.sum(k_terms, axis=0, keepdims=True)

    @pl.when(head == 0)
    def _():
        qsum_ref[...] = jnp.zeros_like(qsum_ref)
        ksum_ref[...] = jnp.zeros_like(ksum_ref)

    qsum_ref[...] += jnp.sum(q_terms * gq_ref[...], axis=1, keepdims=True)
    ksum_ref[...] += jnp.sum(k_terms * gk_ref[...], axis=1, keepdims=True)


def attention_backward(
    lengths, q_rot, k_rot, values, d_attended, lse, q_raw, k_raw, q_scale, k_scale, gain_q, gain_k, cosine, sine
):
    width = q_raw.shape[1]
    heads = width // HEAD_DIM
    gain_spec = pl.BlockSpec((1, HEAD_DIM), lambda h, *_: (0, h))
    return pl.pallas_call(
        attn_bwd_kernel,
        grid_spec=pltpu.PrefetchScalarGridSpec(
            num_scalar_prefetch=1,
            grid=(heads,),
            in_specs=[column_spec()] * 4
            + [pl.BlockSpec((1, LEN, 1), lambda h, *_: (h, 0, 0))]
            + [column_spec()] * 2
            + [whole_spec((LEN, 1))] * 2
            + [gain_spec] * 2
            + [whole_spec((LEN, HEAD_DIM))] * 2,
            out_specs=[column_spec()] * 3 + [whole_spec((LEN, 1))] * 2 + [gain_spec] * 2,
            scratch_shapes=[pltpu.VMEM((LEN, HEAD_DIM), F32)] * 3,
        ),
        out_shape=[jax.ShapeDtypeStruct((LEN, width), F32)] * 2
        + [jax.ShapeDtypeStruct((LEN, width), BF)]
        + [jax.ShapeDtypeStruct((LEN, 1), F32)] * 2
        + [jax.ShapeDtypeStruct((1, width), F32)] * 2,
        compiler_params=pltpu.CompilerParams(vmem_limit_bytes=VMEM_LIMIT),
        cost_estimate=pl.CostEstimate(
            flops=10 * LEN * LEN * width, bytes_accessed=28 * LEN * width, transcendentals=heads * LEN * LEN
        ),
        name="attn_bwd",
    )(lengths, q_rot, k_rot, values, d_attended, lse, q_raw, k_raw, q_scale, k_scale, gain_q, gain_k, cosine, sine)


RTILE = 256


def acts_kernel(len_ref, x_ref, cot_ref, routes_ref, rw_ref, wg_ref, wu_ref, wd_ref, dg_ref, du_ref, ic_ref):
    expert = pl.program_id(0)
    length = len_ref[0]
    for r in range(LEN // RTILE):
        rows = slice(r * RTILE, (r + 1) * RTILE)
        gate = dot(x_ref[rows, :], wg_ref[0])
        up = dot(x_ref[rows, :], wu_ref[0])
        d_inner = dot_nt(cot_ref[rows, :], wd_ref[0])
        position = lax.broadcasted_iota(jnp.int32, (RTILE, 8), 0) + r * RTILE
        named = (routes_ref[rows, :] == expert) & (position < length)
        coef = jnp.sum(jnp.where(named, rw_ref[rows, :], 0.0), axis=1, keepdims=True)
        sig = jax.nn.sigmoid(gate)
        silu = gate * sig
        d_inner = d_inner * coef
        dg_ref[rows, :] = (d_inner * up * (sig + silu * (1.0 - sig))).astype(BF)
        du_ref[rows, :] = (d_inner * silu).astype(BF)
        ic_ref[rows, :] = (silu * up * coef).astype(BF)


def expert_acts(lengths, normed2, cot, routes, route_weights, gate_all, up_all, down_all):
    ff = gate_all.shape[2]
    act_spec = pl.BlockSpec((LEN, ff), lambda e, *_: (0, e))
    top = routes.shape[1]
    return pl.pallas_call(
        acts_kernel,
        grid_spec=pltpu.PrefetchScalarGridSpec(
            num_scalar_prefetch=1,
            grid=(EXPERTS,),
            in_specs=[whole_spec((LEN, D))] * 2
            + [whole_spec((LEN, top))] * 2
            + [pl.BlockSpec((1, D, ff), lambda e, *_: (e, 0, 0))] * 2
            + [pl.BlockSpec((1, ff, D), lambda e, *_: (e, 0, 0))],
            out_specs=[act_spec] * 3,
        ),
        out_shape=[jax.ShapeDtypeStruct((LEN, EXPERTS * ff), BF)] * 3,
        compiler_params=pltpu.CompilerParams(vmem_limit_bytes=VMEM_LIMIT),
        cost_estimate=pl.CostEstimate(
            flops=6 * LEN * D * EXPERTS * ff,
            bytes_accessed=6 * EXPERTS * D * ff + 8 * LEN * D,
            transcendentals=LEN * EXPERTS * ff,
        ),
        name="expert_acts",
    )(lengths, normed2, cot, routes, route_weights, gate_all, up_all, down_all)


NTILE = 512


def back_kernel(dg_ref, du_ref, wg_ref, wu_ref, out_ref, acc):
    expert = pl.program_id(0)

    @pl.when(expert == 0)
    def _():
        acc[...] = jnp.zeros_like(acc)

    for c in range(D // NTILE):
        cols = slice(c * NTILE, (c + 1) * NTILE)
        acc[:, cols] += dot_nt(dg_ref[...], wg_ref[0, cols, :]) + dot_nt(du_ref[...], wu_ref[0, cols, :])

    @pl.when(expert == EXPERTS - 1)
    def _():
        out_ref[...] = acc[...].astype(BF)


def expert_back(d_gate, d_up, gate_all, up_all):
    ff = gate_all.shape[2]
    act_spec = pl.BlockSpec((LEN, ff), lambda e: (0, e))
    return pl.pallas_call(
        back_kernel,
        grid=(EXPERTS,),
        in_specs=[act_spec] * 2 + [pl.BlockSpec((1, D, ff), lambda e: (e, 0, 0))] * 2,
        out_specs=whole_spec((LEN, D)),
        out_shape=jax.ShapeDtypeStruct((LEN, D), BF),
        scratch_shapes=[pltpu.VMEM((LEN, D), F32)],
        compiler_params=pltpu.CompilerParams(vmem_limit_bytes=VMEM_LIMIT),
        cost_estimate=pl.CostEstimate(
            flops=4 * LEN * D * EXPERTS * ff, bytes_accessed=4 * EXPERTS * D * ff + 4 * LEN * D, transcendentals=0
        ),
        name="expert_back",
    )(d_gate, d_up, gate_all, up_all)


def mix_kernel(ic_ref, wd_ref, out_ref, acc):
    expert = pl.program_id(0)

    @pl.when(expert == 0)
    def _():
        acc[...] = jnp.zeros_like(acc)

    for c in range(D // NTILE):
        cols = slice(c * NTILE, (c + 1) * NTILE)
        acc[:, cols] += dot(ic_ref[...], wd_ref[0, :, cols])

    @pl.when(expert == EXPERTS - 1)
    def _():
        out_ref[...] = acc[...].astype(BF)


def expert_mix(inner, down_all):
    ff = down_all.shape[1]
    return pl.pallas_call(
        mix_kernel,
        grid=(EXPERTS,),
        in_specs=[pl.BlockSpec((LEN, ff), lambda e: (0, e)), pl.BlockSpec((1, ff, D), lambda e: (e, 0, 0))],
        out_specs=whole_spec((LEN, D)),
        out_shape=jax.ShapeDtypeStruct((LEN, D), BF),
        scratch_shapes=[pltpu.VMEM((LEN, D), F32)],
        compiler_params=pltpu.CompilerParams(vmem_limit_bytes=VMEM_LIMIT),
        cost_estimate=pl.CostEstimate(
            flops=2 * LEN * D * EXPERTS * ff, bytes_accessed=2 * EXPERTS * D * ff + 2 * LEN * D, transcendentals=0
        ),
        name="expert_mix",
    )(inner, down_all)


def col_grad_kernel(xt_ref, act_ref, out_ref):
    for c in range(D // NTILE):
        rows = slice(c * NTILE, (c + 1) * NTILE)
        out_ref[0, rows, :] = dot(xt_ref[rows, :], act_ref[...]).astype(BF)


def expert_col_grad(x_t, acts, name):
    ff = acts.shape[1] // EXPERTS
    return pl.pallas_call(
        col_grad_kernel,
        grid=(EXPERTS,),
        in_specs=[whole_spec((D, LEN)), pl.BlockSpec((LEN, ff), lambda e: (0, e))],
        out_specs=pl.BlockSpec((1, D, ff), lambda e: (e, 0, 0)),
        out_shape=jax.ShapeDtypeStruct((EXPERTS, D, ff), BF),
        compiler_params=pltpu.CompilerParams(vmem_limit_bytes=VMEM_LIMIT),
        cost_estimate=pl.CostEstimate(
            flops=2 * LEN * D * EXPERTS * ff, bytes_accessed=2 * EXPERTS * D * ff + 2 * LEN * D, transcendentals=0
        ),
        name=name,
    )(x_t, acts)


def row_grad_kernel(count, me_ref, cot_ref, act_ref, keep_ref, away_ref):
    block = D // count
    me = me_ref[0]
    for r in range(count):
        cols = pl.ds(pl.multiple_of((me ^ r) * block, block), block)
        out_ref = away_ref if r % 2 else keep_ref
        out_ref[r // 2, 0] = dot_tn(act_ref[...], cot_ref[:, cols]).astype(BF)


def expert_row_grad(acts, cot, me, count):
    ff = acts.shape[1] // EXPERTS
    block = (ff, D // count)
    return pl.pallas_call(
        functools.partial(row_grad_kernel, count),
        grid_spec=pltpu.PrefetchScalarGridSpec(
            num_scalar_prefetch=1,
            grid=(EXPERTS,),
            in_specs=[whole_spec((LEN, D)), pl.BlockSpec((LEN, ff), lambda e, *_: (0, e))],
            out_specs=[pl.BlockSpec((count // 2, 1) + block, lambda e, *_: (0, e, 0, 0))] * 2,
        ),
        out_shape=[jax.ShapeDtypeStruct((count // 2, EXPERTS) + block, BF)] * 2,
        compiler_params=pltpu.CompilerParams(vmem_limit_bytes=VMEM_LIMIT),
        cost_estimate=pl.CostEstimate(
            flops=2 * LEN * D * EXPERTS * ff, bytes_accessed=2 * EXPERTS * D * ff + 2 * LEN * D, transcendentals=0
        ),
        name="expert_down_grad",
    )(me, cot, acts)


def shards(
    hidden_in,
    norm_gains,
    q_weight,
    k_weight,
    v_weight,
    o_weight,
    gate_weight,
    up_weight,
    down_weight,
    lengths,
    routes,
    route_weights,
    out_grad,
):
    count = lax.axis_size("tensor")
    me = lax.axis_index("tensor")
    own_rows = hidden_in.shape[0]
    width = q_weight.shape[1]
    gain_width = norm_gains.shape[1]
    row_start = me * own_rows
    col_start = me * width
    cosine, sine = rope_tables()
    positions = row_start + jnp.arange(own_rows, dtype=jnp.int32)
    valid_own = (positions < lengths[0]).astype(F32)[:, None]

    dp_count = lax.axis_size("dp")
    me_dp = lax.axis_index("dp")

    x_all = line_gather(hidden_in, count, me)
    rows_local = q_weight.shape[0]
    o_side = jnp.concatenate(jnp.split(o_weight, width // rows_local, axis=0), axis=1)
    qk_part = jnp.concatenate([q_weight, k_weight], axis=1)
    vo_part = jnp.concatenate([v_weight, o_side.reshape(rows_local, width)], axis=1)
    qk_blocks, vo_blocks = cube_gather((qk_part, vo_part), dp_count)
    qk_all = jnp.zeros((D, 2 * width), BF)
    v_all = jnp.zeros((D, width), BF)
    o_all = jnp.zeros((width, D), BF)
    for r in range(dp_count):
        at = (me_dp ^ r) * rows_local
        qk_all = lax.dynamic_update_slice_in_dim(qk_all, qk_blocks[r], at, 0)
        v_all = lax.dynamic_update_slice_in_dim(v_all, vo_blocks[r][:, :width], at, 0)
        o_piece = jnp.concatenate(jnp.split(vo_blocks[r][:, width:], width // rows_local, axis=1), axis=0)
        o_all = lax.dynamic_update_slice_in_dim(o_all, o_piece, at, 1)
    gate_all = lax.all_gather(gate_weight, "dp", axis=1, tiled=True)
    up_all = lax.all_gather(up_weight, "dp", axis=1, tiled=True)
    down_all = lax.all_gather(down_weight, "dp", axis=2, tiled=True)
    gain_piece = jnp.pad(norm_gains.astype(F32), ((0, 4), (0, 128 - gain_width)))
    gains = small_exchange(gain_piece, "tensor", "gather", 1).reshape(count * 8, 128)
    gains = small_exchange(gains, "dp", "gather", 2).reshape(dp_count, count, 8, 128)
    gains = gains[:, :, :4, :gain_width].transpose(2, 0, 1, 3).reshape(4, D)
    cot_all = line_gather(lax.optimization_barrier((out_grad, x_all))[0], count, me)

    gain_q = lax.dynamic_slice_in_dim(gains[1], col_start, width)[None, :]
    gain_k = lax.dynamic_slice_in_dim(gains[2], col_start, width)[None, :]
    unit1, _ = norm_rows(x_all.astype(F32))
    normed1 = (unit1 * gains[0]).astype(BF)
    q_raw = dot(normed1, qk_all[:, :width])
    k_raw = dot(normed1, qk_all[:, width:])
    values = dot(normed1, v_all).astype(BF)
    squares = jnp.stack([jnp.sum(q_raw * q_raw, axis=1), jnp.sum(k_raw * k_raw, axis=1)])
    squares = small_exchange(squares.reshape(-1, 128), "tensor", "sum", 3).reshape(2, LEN)
    scales = lax.rsqrt(squares / D + norm_eps)
    q_scale, k_scale = scales[0][:, None], scales[1][:, None]
    attended, q_rot, k_rot, lse = attention_forward(
        lengths, q_raw, k_raw, values, q_scale, k_scale, gain_q, gain_k, cosine, sine
    )
    branch = line_reduce(dot(attended, o_all).astype(BF), count, me)
    x_own = hidden_in.astype(F32)
    mid = x_own + valid_own * branch
    unit2, scale2 = norm_rows(mid)
    normed2_own, cot_all = lax.optimization_barrier(((unit2 * gains[3]).astype(BF), cot_all))
    normed2 = line_gather(normed2_own, count, me)

    d_gate, d_up, inner = expert_acts(lengths, normed2, cot_all, routes, route_weights, gate_all, up_all, down_all)
    back = expert_back(d_gate, d_up, gate_all, up_all)
    back, d_gate, d_up, inner = lax.optimization_barrier((back, d_gate, d_up, inner))
    d_normed2 = line_reduce(back, count, me)
    normed2_t = normed2.T
    gate_part = expert_col_grad(normed2_t, d_gate, "expert_gate_grad")
    up_part = expert_col_grad(normed2_t, d_up, "expert_up_grad")
    down_part = expert_row_grad(inner, cot_all, me_dp.reshape(1), dp_count)
    d_normed2 = lax.optimization_barrier((d_normed2, gate_part, up_part, down_part))[0]
    gate_grad = lax.psum_scatter(gate_part, "dp", scatter_dimension=1, tiled=True).astype(F32)
    up_grad = lax.psum_scatter(up_part, "dp", scatter_dimension=1, tiled=True).astype(F32)
    down_pair = cube_pair(*down_part, dp_count)

    gain2_term = jnp.sum(d_normed2 * unit2, axis=0)
    d_mid = out_grad.astype(F32) + norm_back(d_normed2, unit2, scale2, gains[3])
    d_branch_own, inner = lax.optimization_barrier(((valid_own * d_mid).astype(BF), inner))
    mixed_part = expert_mix(inner, down_all)
    d_branch = line_gather(d_branch_own, count, me)
    d_branch, mixed_part, down_pair = lax.optimization_barrier((d_branch, mixed_part, down_pair))
    down_half = cube_step(cube_parts(down_pair), dp_count, 0)
    mixed = line_reduce(mixed_part, count, me)
    d_attended = dot_nt(d_branch, o_all).astype(BF)
    o_part = dot_tn(attended, d_branch).astype(BF)
    d_qn, d_kn, d_v, q_sum, k_sum, gainq_term, gaink_term = attention_backward(
        lengths, q_rot, k_rot, values, d_attended, lse, q_raw, k_raw, q_scale, k_scale, gain_q, gain_k, cosine, sine
    )
    sums = jnp.stack([q_sum[:, 0], k_sum[:, 0]]).reshape(-1, 128)
    totals = small_exchange(sums, "tensor", "sum", 4).reshape(2, LEN) / D
    d_q = (q_scale * (d_qn * gain_q) - q_raw * (q_scale * q_scale * totals[0][:, None])).astype(BF)
    d_k = (k_scale * (d_kn * gain_k) - k_raw * (k_scale * k_scale * totals[1][:, None])).astype(BF)
    d_qkv = jnp.concatenate([d_q, d_k, d_v], axis=1)
    d_normed1_part = dot_nt(d_qkv[:, : 2 * width], qk_all) + dot_nt(d_v, v_all)
    d_normed1_low, mixed, down_half = lax.optimization_barrier((d_normed1_part.astype(BF), mixed, down_half))
    down_grad = cube_rest(down_half, dp_count, 1)
    d_normed1 = line_reduce(d_normed1_low, count, me)
    qkv_part = dot_tn(normed1, d_qkv).astype(BF)
    gain1_term = jnp.sum(d_normed1_part * unit1, axis=0)

    zero_row = jnp.zeros((D,), F32)
    gain_terms = jnp.stack(
        [
            gain1_term,
            lax.dynamic_update_slice_in_dim(zero_row, gainq_term[0], col_start, 0),
            lax.dynamic_update_slice_in_dim(zero_row, gaink_term[0], col_start, 0),
            gain2_term,
        ],
        axis=0,
    )
    pieces = gain_terms.reshape(4, dp_count, count, gain_width).transpose(2, 1, 0, 3)
    pieces = jnp.pad(pieces, ((0, 0), (0, 0), (0, 4), (0, 128 - gain_width))).reshape(count, dp_count * 8, 128)
    pieces = small_exchange(pieces, "tensor", "scatter", 5).reshape(dp_count, 8, 128)
    gains_grad = small_exchange(pieces, "dp", "scatter", 6)[:4, :gain_width]

    blocks = []
    for r in range(dp_count):
        at = (me_dp ^ r) * rows_local
        o_piece = lax.dynamic_slice_in_dim(o_part, at, rows_local, 1)
        o_piece = jnp.concatenate(jnp.split(o_piece, width // rows_local, axis=0), axis=1)
        blocks.append(jnp.concatenate([lax.dynamic_slice_in_dim(qkv_part, at, rows_local, 0), o_piece], axis=1))
    qkvo_pair = cube_pair(jnp.stack(blocks[0::2]), jnp.stack(blocks[1::2]), dp_count)
    qkvo_grad = cube_rest(cube_parts(qkvo_pair), dp_count)
    q_grad, k_grad, v_grad, o_grad = jnp.split(qkvo_grad, [width, 2 * width, 3 * width], axis=1)
    o_grad = jnp.concatenate(jnp.split(o_grad, width // rows_local, axis=1), axis=0)
    block_out = (mid + mixed).astype(BF)
    unit1_own, scale1_own = norm_rows(x_own)
    input_grad = d_mid + norm_back(d_normed1, unit1_own, scale1_own, gains[0])
    return (
        block_out,
        input_grad,
        gains_grad,
        q_grad,
        k_grad,
        v_grad,
        o_grad,
        gate_grad,
        up_grad,
        down_grad,
    )


def solution(mesh):
    placed = (
        P(("dp", "tensor"), None),
        P(None, ("dp", "tensor")),
        P("dp", "tensor"),
        P("dp", "tensor"),
        P("dp", "tensor"),
        P("tensor", "dp"),
        P(None, "dp", "tensor"),
        P(None, "dp", "tensor"),
        P(None, "tensor", "dp"),
        P("dp"),
        P("dp", None),
        P("dp", None),
        P(("dp", "tensor"), None),
    )
    return jax.shard_map(
        shards,
        mesh=mesh,
        in_specs=placed,
        out_specs=(
            P(("dp", "tensor"), None),
            P(("dp", "tensor"), None),
            P(None, ("dp", "tensor")),
            P("dp", "tensor"),
            P("dp", "tensor"),
            P("dp", "tensor"),
            P("tensor", "dp"),
            P(None, "dp", "tensor"),
            P(None, "dp", "tensor"),
            P(None, "tensor", "dp"),
        ),
        check_vma=False,
    )
```

time: 3080 us -> 1110 us (0.36)
  waiting for transfers between devices: 1880 us -> 344 us
  matrix products: 753 us -> 53.8 us
  Pallas kernels: 0 us -> 351 us
  local copies, waits for them, and re-layouts: 276 us -> 88.4 us
  starting transfers between devices: 1.34 us -> 122 us
  blocking collectives: 60.3 us -> 0 us
  other arithmetic: 89 us -> 121 us
    reduce_scatter x11 -> x2, waiting for transfers between devices: 1270 us -> 0.01 us  [the longest x1 0.01 us: shards(): lax.psum_scatter(gate_part, 'dp', scatter_dimension=1, tiled=True)]
    dot_general x162 -> x9, matrix products: 753 us -> 53.8 us  [the longest x3 21.1 us: dot_nt(): lax.dot_general(left, right, (((1,), (1,)), ((), ())), preferred_element_...]
    all_gather x11 -> x3, waiting for transfers between devices: 600 us -> 0.01 us  [the longest x1 0.01 us: shards(): gate_all = lax.all_gather(gate_weight, 'dp', axis=1, tiled=True)]
    pallas_call x0 -> x14, Pallas kernels: none -> 351 us  [the longest x6 109 us: small_exchange(): pl.pallas_call(functools.partial(small_kernel, axis, count, mode), in_spe...]
    ppermute x0 -> x64, waiting for transfers between devices: none -> 342 us  [the longest x12 108 us: line_gather(): lax.ppermute(from_right[-1], 'tensor', leftward[:count - step])]
    dynamic_update_slice x67 -> x24, local copies, waits for them, and re-layouts: 132 us -> 10.1 us  [the longest x8 5.77 us: shards(): lax.dynamic_update_slice_in_dim(v_all, vo_blocks[r][:, :width], at, 0)]
    ppermute x0 -> x64, starting transfers between devices: none -> 122 us  [the longest x12 49.6 us: line_reduce(): left = lax.ppermute(to_right, 'tensor', rightward)]
    while x320 -> x0, local copies, waits for them, and re-layouts: 53.2 us -> none
  transfers between devices with their start and end apart: 23 -> 69, of which waited for: 18 -> 28; matrix products, arithmetic and copies ran while one was open for 31% -> 22% of each run, Pallas kernels for 0% -> 20%
where the time goes in v1:
time: 1110 us; the launch traced here: 1100 us
  Pallas kernels  351 us (32%)
  waiting for transfers between devices  344 us (31%)
  starting transfers between devices  122 us (11%)
  other arithmetic  121 us (11%)
  local copies, waits for them, and re-layouts  88.4 us (8%)
  matrix products  53.8 us (5%)
  between operations  17.1 us (2%)
    pallas_call x6, Pallas kernels, small_exchange(): pl.pallas_call(functools.partial(small_kernel, axis, count, mode), in_spe...  109 us
    ppermute x12, waiting for transfers between devices, line_gather(): lax.ppermute(from_right[-1], 'tensor', leftward[:count - step])  108 us
    ppermute x12, waiting for transfers between devices, line_reduce(): left = lax.ppermute(to_right, 'tensor', rightward)  104 us
    ppermute x16, waiting for transfers between devices, flip(): return lax.ppermute(x, 'dp', [(i, i ^ 1 << bit) for i in range(count)])  73.5 us
    pallas_call x1, Pallas kernels, expert_acts(): pl.pallas_call(acts_kernel, grid_spec=pltpu.PrefetchScalarGridSpec(num_sc...  62.8 us
    pallas_call x2, Pallas kernels, expert_col_grad(): pl.pallas_call(col_grad_kernel, grid=(EXPERTS,), in_specs=[whole_spec((D,...  49.7 us
    ppermute x12, starting transfers between devices, line_reduce(): left = lax.ppermute(to_right, 'tensor', rightward)  49.6 us
    pallas_call x1, Pallas kernels, expert_back(): pl.pallas_call(back_kernel, grid=(EXPERTS,), in_specs=[act_spec] * 2 + [p...  43.2 us
  transfers between devices with their start and end apart: 69, of which 28 were waited for; matrix products, arithmetic and copies ran while one was open for 22% of the time, Pallas kernels for 20%

profile of v1, /device:TPU:0, one launch (start us, length us, event | category | flops | bytes accessed | tf_op | source)
XLA Modules:
  0.0 1097.5 jit_solution(1916993005735660285)
XLA Ops:
  20.7 23.2 %small_gather_1.1 = f32[4,8,128]{2,1,0:T(8,128)} custom-call(f32[8,128]{1,0:T(8,128)} %pad_convert_fusion.x_ref), custom_call_target="tpu_custom_call" | custom-call | tf_op jit(solution)/shard_map/small_gather_1/pallas_call | solution.py:129
  85.9 20.9 %collective-permute-done.7 = bf16[2,256,1024]{2,1,0:T(8,128)(2,1)} collective-permute-done((bf16[2,256,1024]{2,1,0:T(8,128)(2,1)}, bf16[2,256,1024]{2,1,0:T(8,128)(2,1)}, u32[]{:S(2)}, u32[]{:S(2)}) %collective-permute-start.7) | collective-permute-done | bytes 1048608 | tf_op jit(solution)/shard_map/ppermute | solution.py:145
  141.7 31.0 %small_sum_3.1 = f32[16,128]{1,0:T(8,128)} custom-call(f32[16,128]{1,0:T(8,128)} %reshape.203.x_ref), custom_call_target="tpu_custom_call" | custom-call | tf_op jit(solution)/shard_map/small_sum_3/pallas_call | solution.py:129
  190.0 15.9 %attn_fwd.1 = (bf16[1024,512]{1,0:T(8,128)(2,1)}, bf16[1024,512]{1,0:T(8,128)(2,1)}, bf16[1024,512]{1,0:T(8,128)(2,1)}, f32[4,1024,1]{2,1,0:T(8,128)}) custom-call(s32[1]{0:T(128)} %copy.107.len_ref, f32[1024,512]{1,0:T(8,128)} %copy.42.q_ref, f32[1024,512]{1,0:T(8,128)} %copy.43.k_ref, bf16[1024,512]{1,0:T(8,128)(2,1)} %convolution_convert_fusion.4.v_ref, ...), custom_call_target="tpu_custom_call" | custom-call | flops 2147483648 | bytes 8388608 | tf_op jit(solution)/shard_map/attn_fwd/pallas_call | solution.py:246
  219.0 18.3 %collective-permute-done.12 = bf16[256,2048]{1,0:T(8,128)(2,1)S(1)} collective-permute-done((bf16[256,2048]{1,0:T(8,128)(2,1)S(1)}, bf16[256,2048]{1,0:T(8,128)(2,1)S(1)}, u32[]{:S(2)}, u32[]{:S(2)}) %collective-permute-start.12) | collective-permute-done | bytes 1048608 | tf_op jit(solution)/shard_map/ppermute | solution.py:87
  244.1 15.7 %collective-permute-done.18 = bf16[256,2048]{1,0:T(8,128)(2,1)} collective-permute-done((bf16[256,2048]{1,0:T(8,128)(2,1)S(1)}, bf16[256,2048]{1,0:T(8,128)(2,1)}, u32[]{:S(2)}, u32[]{:S(2)}) %collective-permute-start.18) | collective-permute-done | bytes 1048608 | tf_op jit(solution)/shard_map/ppermute | solution.py:63
  262.7 17.5 %collective-permute-done.13 = bf16[256,2048]{1,0:T(8,128)(2,1)} collective-permute-done((bf16[256,2048]{1,0:T(8,128)(2,1)}, bf16[256,2048]{1,0:T(8,128)(2,1)}, u32[]{:S(2)}, u32[]{:S(2)}) %collective-permute-start.13) | collective-permute-done | bytes 1048608 | tf_op jit(solution)/shard_map/ppermute | solution.py:87
  312.6 22.5 %collective-permute-done.17 = bf16[256,2048]{1,0:T(8,128)(2,1)S(1)} collective-permute-done((bf16[256,2048]{1,0:T(8,128)(2,1)S(1)}, bf16[256,2048]{1,0:T(8,128)(2,1)S(1)}, u32[]{:S(2)}, u32[]{:S(2)}) %collective-permute-start.17) | collective-permute-done | bytes 1048608 | tf_op jit(solution)/shard_map/ppermute | solution.py:88
  344.1 17.7 %collective-permute-done.25 = bf16[256,2048]{1,0:T(8,128)(2,1)S(1)} collective-permute-done((bf16[256,2048]{1,0:T(8,128)(2,1)S(1)}, bf16[256,2048]{1,0:T(8,128)(2,1)S(1)}, u32[]{:S(2)}, u32[]{:S(2)}) %collective-permute-start.25) | collective-permute-done | bytes 1048608 | tf_op jit(solution)/shard_map/ppermute | solution.py:64
  364.8 20.1 %collective-permute-done.26 = bf16[256,2048]{1,0:T(8,128)(2,1)} collective-permute-done((bf16[256,2048]{1,0:T(8,128)(2,1)S(1)}, bf16[256,2048]{1,0:T(8,128)(2,1)}, u32[]{:S(2)}, u32[]{:S(2)}) %collective-permute-start.26) | collective-permute-done | bytes 1048608 | tf_op jit(solution)/shard_map/ppermute | solution.py:64
  420.1 62.8 %expert_acts.1 = (bf16[1024,4096]{1,0:T(8,128)(2,1)}, bf16[1024,4096]{1,0:T(8,128)(2,1)}, bf16[1024,4096]{1,0:T(8,128)(2,1)}) custom-call(s32[1]{0:T(128)} %copy.107.len_ref, bf16[1024,2048]{1,0:T(8,128)(2,1)} %select_dynamic-update-slice_fusion.3.x_ref, bf16[1024,2048]{1,0:T(8,128)(2,1)} %copy-done.31, s32[1024,8]{1,0:T(8,128)} %copy.46.routes_ref, ...), custom_call_target="tpu_custom_call" | custom-call | flops 51539607552 | bytes 67108864 | tf_op jit(solution)/shard_map/expert_acts/pallas_call | solution.py:367
  483.0 43.2 %expert_back.1 = bf16[1024,2048]{1,0:T(8,128)(2,1)} custom-call(bf16[1024,4096]{1,0:T(8,128)(2,1)} %get-tuple-element.55.dg_ref.act_ref, bf16[1024,4096]{1,0:T(8,128)(2,1)} %get-tuple-element.56.du_ref.act_ref, bf16[16,2048,256]{2,1,0:T(8,128)(2,1)} %all-gather.4.cloned.1.call-done.wg_ref, bf16[16,2048,256]{2,1,0:T(8,128)(2,1)} %all-gather.6.cloned.1.call-done.wu_ref), custom_call_target="tpu_custom_call" | custom-call | flops 34359738368 | bytes 41943040 | tf_op jit(solution)/shard_map/expert_back/pallas_call | solution.py:411
  526.2 24.8 %expert_gate_grad.1 = bf16[16,2048,256]{2,1,0:T(8,128)(2,1)} custom-call(bf16[2048,1024]{1,0:T(8,128)(2,1)} %copy.48.xt_ref, bf16[1024,4096]{1,0:T(8,128)(2,1)} %get-tuple-element.55.dg_ref.act_ref), custom_call_target="tpu_custom_call" | custom-call | flops 17179869184 | bytes 20971520 | tf_op jit(solution)/shard_map/expert_gate_grad/pallas_call | solution.py:467
  555.1 17.7 %collective-permute-done.30 = bf16[256,2048]{1,0:T(8,128)(2,1)S(1)} collective-permute-done((bf16[256,2048]{1,0:T(8,128)(2,1)S(1)}, bf16[256,2048]{1,0:T(8,128)(2,1)S(1)}, u32[]{:S(2)}, u32[]{:S(2)}) %collective-permute-start.30) | collective-permute-done | bytes 1048608 | tf_op jit(solution)/shard_map/ppermute | solution.py:87
  577.7 16.0 %collective-permute-done.31 = bf16[256,2048]{1,0:T(8,128)(2,1)S(1)} collective-permute-done((bf16[256,2048]{1,0:T(8,128)(2,1)S(1)}, bf16[256,2048]{1,0:T(8,128)(2,1)S(1)}, u32[]{:S(2)}, u32[]{:S(2)}) %collective-permute-start.31) | collective-permute-done | bytes 1048608 | tf_op jit(solution)/shard_map/ppermute | solution.py:87
  596.3 26.0 %expert_down_grad.1 = (bf16[4,16,256,256]{3,2,1,0:T(8,128)(2,1)}, bf16[4,16,256,256]{3,2,1,0:T(8,128)(2,1)}) custom-call(s32[1]{0:T(128)} %bitcast.28.me_ref, bf16[1024,2048]{1,0:T(8,128)(2,1)} %copy-done.31, bf16[1024,4096]{1,0:T(8,128)(2,1)} %get-tuple-element.62.act_ref.ic_ref), custom_call_target="tpu_custom_call" | custom-call | flops 17179869184 | bytes 20971520 | tf_op jit(solution)/shard_map/expert_down_grad/pallas_call | solution.py:493
  631.5 24.9 %expert_up_grad.1 = bf16[16,2048,256]{2,1,0:T(8,128)(2,1)} custom-call(bf16[2048,1024]{1,0:T(8,128)(2,1)} %copy.48.xt_ref, bf16[1024,4096]{1,0:T(8,128)(2,1)} %get-tuple-element.56.du_ref.act_ref), custom_call_target="tpu_custom_call" | custom-call | flops 17179869184 | bytes 20971520 | tf_op jit(solution)/shard_map/expert_up_grad/pallas_call | solution.py:467
  669.6 20.3 %collective-permute-done.37 = bf16[256,2048]{1,0:T(8,128)(2,1)} collective-permute-done((bf16[256,2048]{1,0:T(8,128)(2,1)S(1)}, bf16[256,2048]{1,0:T(8,128)(2,1)}, u32[]{:S(2)}, u32[]{:S(2)}) %collective-permute-start.37) | collective-permute-done | bytes 1048608 | tf_op jit(solution)/shard_map/ppermute | solution.py:64
  695.7 20.5 %collective-permute-done.38 = bf16[256,2048]{1,0:T(8,128)(2,1)} collective-permute-done((bf16[256,2048]{1,0:T(8,128)(2,1)}, bf16[256,2048]{1,0:T(8,128)(2,1)}, u32[]{:S(2)}, u32[]{:S(2)}) %collective-permute-start.38) | collective-permute-done | bytes 1048608 | tf_op jit(solution)/shard_map/ppermute | solution.py:64
  717.5 26.3 %expert_mix.1 = bf16[1024,2048]{1,0:T(8,128)(2,1)} custom-call(bf16[1024,4096]{1,0:T(8,128)(2,1)} %get-tuple-element.62.act_ref.ic_ref, bf16[16,256,2048]{2,1,0:T(8,128)(2,1)} %all-gather.8.cloned.1.call-done.wd_ref), custom_call_target="tpu_custom_call" | custom-call | flops 17179869184 | bytes 20971520 | tf_op jit(solution)/shard_map/expert_mix/pallas_call | solution.py:444
  767.1 18.6 %attn_bwd.1 = (f32[1024,512]{1,0:T(8,128)}, f32[1024,512]{1,0:T(8,128)}, bf16[1024,512]{1,0:T(8,128)(2,1)}, f32[1024,1]{1,0:T(8,128)}, f32[1024,1]{1,0:T(8,128)}, /*index=5*/f32[1,512]{1,0:T(1,128)}, f32[1,512]{1,0:T(1,128)}) custom-call(s32[1]{0:T(128)} %copy.107.len_ref, bf16[1024,512]{1,0:T(8,128)(2,1)} %get-tuple-element.46.qr_ref, ...), custom_call_target="tpu_custom_call" | custom-call | flops 5368709120 | bytes 14680064 | tf_op jit(solution)/shard_map/attn_bwd/pallas_call | solution.py:315
  788.8 21.4 %small_sum_4.1 = f32[16,128]{1,0:T(8,128)} custom-call(f32[16,128]{1,0:T(8,128)} %reshape.205.x_ref), custom_call_target="tpu_custom_call" | custom-call | tf_op jit(solution)/shard_map/small_sum_4/pallas_call | solution.py:129
  943.0 18.0 %small_scatter_5.1 = f32[64,128]{1,0:T(8,128)} custom-call(f32[4,64,128]{2,1,0:T(8,128)} %pad_bitcast_fusion.x_ref), custom_call_target="tpu_custom_call" | custom-call | tf_op jit(solution)/shard_map/small_scatter_5/pallas_call | solution.py:129
  1007.9 15.6 %collective-permute-done.62 = bf16[1,8,256,256]{3,2,1,0:T(8,128)(2,1)S(1)} collective-permute-done((bf16[1,8,256,256]{3,2,1,0:T(8,128)(2,1)S(1)}, bf16[1,8,256,256]{3,2,1,0:T(8,128)(2,1)S(1)}, u32[]{:S(2)}, u32[]{:S(2)}) %collective-permute-start.62) | collective-permute-done | bytes 1048608 | tf_op jit(solution)/shard_map/ppermute | solution.py:145
  (521 shorter events, 521.6 us)
Async XLA Ops:
  7.2 412.9 %all-gather.4.cloned.1.call-start = ((), (), s32[]{:S(2)}) async-start(), calls=%async_computation.2 | async-start | bytes 18874368 | tf_op jit(solution)/shard_map/all_gather | solution.py:554
  7.9 412.2 %all-gather.6.cloned.1.call-start = ((), (), s32[]{:S(2)}) async-start(), calls=%async_computation.3 | async-start | bytes 18874368 | tf_op jit(solution)/shard_map/all_gather | solution.py:555
  8.7 411.4 %all-gather.8.cloned.1.call-start = ((), (), s32[]{:S(2)}) async-start(), calls=%async_computation.4 | async-start | bytes 18874368 | tf_op jit(solution)/shard_map/all_gather | solution.py:556
  9.5 1072.9 %reduce-scatter.3.cloned.1.call-start = ((), (), s32[]{:S(2)}) async-start(), calls=%async_computation.5 | async-start | bytes 18874368 | tf_op jit(solution)/shard_map/reduce_scatter | solution.py:593
  9.5 59.1 %collective-permute-start = (bf16[256,2048]{1,0:T(8,128)(2,1)S(1)}, bf16[256,2048]{1,0:T(8,128)(2,1)}, u32[]{:S(2)}, u32[]{:S(2)}) collective-permute-start(bf16[256,2048]{1,0:T(8,128)(2,1)S(1)} %copy-done.12), channel_id=1, source_target_pairs={{0,1},{1,2},{2,3},{4,5},{5,6},{6,7},{8,9},{9,10},{10,11},{12,13},{... | collective-permute-start | bytes 3145736 | tf_op jit(solution)/shard_map/ppermute | solution.py:63
  18.5 43.6 %collective-permute-start.9 = (bf16[1,256,1024]{2,1,0:T(8,128)(2,1)S(1)}, bf16[1,256,1024]{2,1,0:T(8,128)(2,1)S(1)}, u32[]{:S(2)}, u32[]{:S(2)}) collective-permute-start(bf16[1,256,1024]{2,1,0:T(8,128)(2,1)S(1)} %maximum_bitcast_fusion.8), channel_id=1, source_target_pairs={{0,16},{4,20},{8,24},{12,28},{16,0},{20,4},{24,8},{28,12},{1,17},{... | collective-permute-start | bytes 1572872 | tf_op jit(solution)/shard_map/ppermute | solution.py:145
  59.3 47.5 %collective-permute-start.7 = (bf16[2,256,1024]{2,1,0:T(8,128)(2,1)}, bf16[2,256,1024]{2,1,0:T(8,128)(2,1)}, u32[]{:S(2)}, u32[]{:S(2)}) collective-permute-start(bf16[2,256,1024]{2,1,0:T(8,128)(2,1)} %pad_maximum_fusion.5), channel_id=1, source_target_pairs={{0,16},{4,20},{8,24},{12,28},{16,0},{20,4},{24,8},{28,12},{1,17},{... | collective-permute-start | bytes 3145736 | tf_op jit(solution)/shard_map/ppermute | solution.py:145
  62.3 48.7 %collective-permute-start.10 = (bf16[2,256,1024]{2,1,0:T(8,128)(2,1)S(1)}, bf16[2,256,1024]{2,1,0:T(8,128)(2,1)S(1)}, u32[]{:S(2)}, u32[]{:S(2)}) collective-permute-start(bf16[2,256,1024]{2,1,0:T(8,128)(2,1)S(1)} %pad_maximum_fusion.6), channel_id=1, source_target_pairs={{0,8},{4,12},{8,0},{12,4},{16,24},{20,28},{24,16},{28,20},{1,9},{5... | collective-permute-start | bytes 3145736 | tf_op jit(solution)/shard_map/ppermute | solution.py:145
  68.6 45.0 %collective-permute-start.4 = (bf16[256,2048]{1,0:T(8,128)(2,1)}, bf16[256,2048]{1,0:T(8,128)(2,1)S(1)}, u32[]{:S(2)}, u32[]{:S(2)}) collective-permute-start(bf16[256,2048]{1,0:T(8,128)(2,1)} %collective-permute-done), channel_id=1, source_target_pairs={{1,2},{2,3},{5,6},{6,7},{9,10},{10,11},{13,14},{14,15},{17,18},{18... | collective-permute-start | bytes 3145736 | tf_op jit(solution)/shard_map/ppermute | solution.py:63
  112.8 63.3 %collective-permute-start.11 = (bf16[4,256,1024]{2,1,0:T(8,128)(2,1)}, bf16[4,256,1024]{2,1,0:T(8,128)(2,1)}, u32[]{:S(2)}, u32[]{:S(2)}) collective-permute-start(bf16[4,256,1024]{2,1,0:T(8,128)(2,1)} %pad_maximum_fusion.3), channel_id=1, source_target_pairs={{0,4},{4,0},{8,12},{12,8},{16,20},{20,16},{24,28},{28,24},{1,5},{5... | collective-permute-start | bytes 6291464 | tf_op jit(solution)/shard_map/ppermute | solution.py:145
  118.1 99.6 %collective-permute-start.19 = (bf16[256,2048]{1,0:T(8,128)(2,1)S(1)}, bf16[256,2048]{1,0:T(8,128)(2,1)}, u32[]{:S(2)}, u32[]{:S(2)}) collective-permute-start(bf16[256,2048]{1,0:T(8,128)(2,1)S(1)} %copy-done.18), channel_id=1, source_target_pairs={{1,0},{2,1},{3,2},{5,4},{6,5},{7,6},{9,8},{10,9},{11,10},{13,12},{... | collective-permute-start | bytes 3145736 | tf_op jit(solution)/shard_map/ppermute | solution.py:64
  213.8 45.9 %collective-permute-start.18 = (bf16[256,2048]{1,0:T(8,128)(2,1)S(1)}, bf16[256,2048]{1,0:T(8,128)(2,1)}, u32[]{:S(2)}, u32[]{:S(2)}) collective-permute-start(bf16[256,2048]{1,0:T(8,128)(2,1)S(1)} %copy-done.18), channel_id=1, source_target_pairs={{0,1},{1,2},{2,3},{4,5},{5,6},{6,7},{8,9},{9,10},{10,11},{12,13},{... | collective-permute-start | bytes 3145736 | tf_op jit(solution)/shard_map/ppermute | solution.py:63
  216.1 46.6 %collective-permute-start.15 = (bf16[256,2048]{1,0:T(8,128)(2,1)S(1)}, bf16[256,2048]{1,0:T(8,128)(2,1)}, u32[]{:S(2)}, u32[]{:S(2)}) collective-permute-start(bf16[256,2048]{1,0:T(8,128)(2,1)S(1)} %get-tuple-element.145), channel_id=1, source_target_pairs={{3,2},{7,6},{11,10},{15,14},{19,18},{23,22},{27,26},{31,30}} | collective-permute-start | bytes 3145736 | tf_op jit(solution)/shard_map/ppermute | solution.py:88
  217.7 43.7 %collective-permute-start.20 = (bf16[256,2048]{1,0:T(8,128)(2,1)}, bf16[256,2048]{1,0:T(8,128)(2,1)}, u32[]{:S(2)}, u32[]{:S(2)}) collective-permute-start(bf16[256,2048]{1,0:T(8,128)(2,1)} %collective-permute-done.19), channel_id=1, source_target_pairs={{1,0},{2,1},{5,4},{6,5},{9,8},{10,9},{13,12},{14,13},{17,16},{18,1... | collective-permute-start | bytes 3145736 | tf_op jit(solution)/shard_map/ppermute | solution.py:64
  238.6 41.6 %collective-permute-start.13 = (bf16[256,2048]{1,0:T(8,128)(2,1)}, bf16[256,2048]{1,0:T(8,128)(2,1)}, u32[]{:S(2)}, u32[]{:S(2)}) collective-permute-start(bf16[256,2048]{1,0:T(8,128)(2,1)} %add_convert_fusion.22), channel_id=1, source_target_pairs={{0,1},{1,2},{4,5},{5,6},{8,9},{9,10},{12,13},{13,14},{16,17},{17,1... | collective-permute-start | bytes 3145736 | tf_op jit(solution)/shard_map/ppermute | solution.py:87
  551.0 535.4 %reduce-scatter.5.cloned.1.call-start = ((), (), s32[]{:S(2)}) async-start(), calls=%async_computation.6 | async-start | bytes 18874368 | tf_op jit(solution)/shard_map/reduce_scatter | solution.py:594
  622.3 130.1 %collective-permute-start.42 = (bf16[4,16,256,256]{3,2,1,0:T(8,128)(2,1)}, bf16[4,16,256,256]{3,2,1,0:T(8,128)(2,1)}, u32[]{:S(2)}, u32[]{:S(2)}) collective-permute-start(bf16[4,16,256,256]{3,2,1,0:T(8,128)(2,1)} %get-tuple-element.59), channel_id=1, source_target_pairs={{0,4},{4,0},{8,12},{12,8},{16,20},{20,16},{24,28},{28,24},{1,5},{5... | collective-permute-start | bytes 25165832 | tf_op jit(solution)/shard_map/ppermute | solution.py:145
  695.0 48.9 %collective-permute-start.40 = (bf16[256,2048]{1,0:T(8,128)(2,1)}, bf16[256,2048]{1,0:T(8,128)(2,1)S(1)}, u32[]{:S(2)}, u32[]{:S(2)}) collective-permute-start(bf16[256,2048]{1,0:T(8,128)(2,1)} %collective-permute-done.36), channel_id=1, source_target_pairs={{1,2},{2,3},{5,6},{6,7},{9,10},{10,11},{13,14},{14,15},{17,18},{18... | collective-permute-start | bytes 3145736 | tf_op jit(solution)/shard_map/ppermute | solution.py:63
  813.3 44.9 %collective-permute-start.43 = (bf16[256,2048]{1,0:T(8,128)(2,1)}, bf16[256,2048]{1,0:T(8,128)(2,1)}, u32[]{:S(2)}, u32[]{:S(2)}) collective-permute-start(bf16[256,2048]{1,0:T(8,128)(2,1)} %get-tuple-element.136), channel_id=1, source_target_pairs={{0,1},{4,5},{8,9},{12,13},{16,17},{20,21},{24,25},{28,29}} | collective-permute-start | bytes 3145736 | tf_op jit(solution)/shard_map/ppermute | solution.py:87
  817.5 55.3 %collective-permute-start.46 = (bf16[256,2048]{1,0:T(8,128)(2,1)}, bf16[256,2048]{1,0:T(8,128)(2,1)}, u32[]{:S(2)}, u32[]{:S(2)}) collective-permute-start(bf16[256,2048]{1,0:T(8,128)(2,1)} %get-tuple-element.137), channel_id=1, source_target_pairs={{3,2},{7,6},{11,10},{15,14},{19,18},{23,22},{27,26},{31,30}} | collective-permute-start | bytes 3145736 | tf_op jit(solution)/shard_map/ppermute | solution.py:88
  822.4 88.3 %collective-permute-start.50 = (bf16[2,8,256,256]{3,2,1,0:T(8,128)(2,1)}, bf16[2,8,256,256]{3,2,1,0:T(8,128)(2,1)}, u32[]{:S(2)}, u32[]{:S(2)}) collective-permute-start(bf16[2,8,256,256]{3,2,1,0:T(8,128)(2,1)} %stack.111), channel_id=1, source_target_pairs={{0,16},{4,20},{8,24},{12,28},{16,0},{20,4},{24,8},{28,12},{1,17},{... | collective-permute-start | bytes 6291464 | tf_op jit(solution)/shard_map/ppermute | solution.py:145
  825.7 85.0 %collective-permute-start.49 = (bf16[2,8,256,256]{3,2,1,0:T(8,128)(2,1)}, bf16[2,8,256,256]{3,2,1,0:T(8,128)(2,1)}, u32[]{:S(2)}, u32[]{:S(2)}) collective-permute-start(bf16[2,8,256,256]{3,2,1,0:T(8,128)(2,1)} %pad_maximum_fusion.4), channel_id=1, source_target_pairs={{0,8},{4,12},{8,0},{12,4},{16,24},{20,28},{24,16},{28,20},{1,9},{5... | collective-permute-start | bytes 6291464 | tf_op jit(solution)/shard_map/ppermute | solution.py:145
  865.5 105.3 %collective-permute-start.57 = (bf16[4,256,2048]{1,2,0:T(8,128)(2,1)}, bf16[4,256,2048]{1,2,0:T(8,128)(2,1)}, u32[]{:S(2)}, u32[]{:S(2)}) collective-permute-start(bf16[4,256,2048]{1,2,0:T(8,128)(2,1)} %pad_maximum_fusion), channel_id=1, source_target_pairs={{0,4},{4,0},{8,12},{12,8},{16,20},{20,16},{24,28},{28,24},{1,5},{5... | collective-permute-start | bytes 12582920 | tf_op jit(solution)/shard_map/ppermute | solution.py:145
  983.1 46.9 %collective-permute-start.58 = (bf16[2,128,2048]{1,2,0:T(8,128)(2,1)S(1)}, bf16[2,128,2048]{1,2,0:T(8,128)(2,1)S(1)}, u32[]{:S(2)}, u32[]{:S(2)}) collective-permute-start(bf16[2,128,2048]{1,2,0:T(8,128)(2,1)S(1)} %pad_maximum_fusion.7), channel_id=1, source_target_pairs={{0,8},{4,12},{8,0},{12,4},{16,24},{20,28},{24,16},{28,20},{1,9},{5... | collective-permute-start | bytes 3145736 | tf_op jit(solution)/shard_map/ppermute | solution.py:145
  (148 other events, 2257.9 us)
Sparse Core Ops, SparseCore 0:
  9.9 123.5 all-gather.3
  135.3 89.5 all-gather.5
  226.8 93.0 all-gather.7
  551.1 114.5 reduce-scatter.2
  691.8 118.7 reduce-scatter.4
